TPU v7x, 32 devices: a whole 2x2x4 slice. The times are simulated.
32 devices in a mesh: seq: 8 (over z, x), hid: 4 (over y, core).
Axes of the slice: x: 2, y: 2, z: 4, core: 2. Of those that a mesh axis runs over, the one named last changes fastest.
Arguments:
- hidden: bfloat16 [8192, 4096], P('seq', 'hid'), may hold values from -40 to 40, as said below
- seg_ids: int32 [8192], P('seq'), may hold values from 0 to 31, as said below
- lengths: int32 [32], replicated, may hold values from 64 to 4096, as said below
- owner_slot: int32 [32], replicated, may hold values from 0 to 31, each once
- pool_bias: float32 [4096], P('hid'), may hold values from -3 to 3
Outputs:
- pooled: bfloat16 [32, 4096], P('seq', 'hid')
Inputs may be any that keep to these rules, and one draw needn't show every extreme that they name: `hidden`: float values; each feature's scale differs. `seg_ids`: never falls along the stream; document d occupies exactly lengths[d] consecutive tokens, documents in order. `lengths`: they sum to 8192; one of them is exactly 4096; the first 16 documents each have 1024 // 16 tokens and so fill the first index's tokens; hence at most 16 documents end within one index's tokens, and the first index has exactly 16. `owner_slot`: each row number once.
All inputs are finite; a program needn't handle non-finite values.
Results may differ from a plain program's by a relative error of at most 0.001.
Values may be sent and summed in bfloat16 or wider, within the bound.
A program may use at most 64 MiB of HBM per device.

v0:
```python
import jax
import jax.numpy as jnp
from jax import lax
from jax.sharding import PartitionSpec as P


def local(hidden, seg_ids, lengths, owner_slot, pool_bias):
    tok_rows, width_part = hidden.shape
    doc_count = lengths.shape[0]
    seq_count = lax.axis_size("seq")
    per_owner = doc_count // seq_count
    features = width_part * lax.axis_size("hid")
    doc_iota = lax.broadcasted_iota(jnp.int32, (1, doc_count), 1)
    in_doc = (seg_ids[:, None] == doc_iota).astype(jnp.int32)
    token_row = jnp.sum(in_doc * owner_slot[None, :], axis=1)
    row_iota = lax.broadcasted_iota(jnp.int32, (doc_count, 1), 0)
    routed = (owner_slot[None, :] == row_iota).astype(jnp.int32)
    row_length = jnp.sum(routed * lengths[None, :], axis=1).astype(jnp.float32)
    wanted = lax.broadcasted_iota(jnp.int32, (per_owner * lax.axis_size("seq"), 1), 0)
    picker = (wanted == token_row[None, :]).astype(jnp.bfloat16)
    totals = lax.psum_scatter(
        jnp.dot(picker, hidden, preferred_element_type=jnp.float32),
        "seq",
        scatter_dimension=0,
        tiled=True,
    )
    my_length = lax.dynamic_slice_in_dim(row_length, lax.axis_index("seq") * per_owner, per_owner)
    averages = totals / my_length[:, None] + pool_bias[None, :]
    energy = lax.psum(jnp.sum(averages * averages, axis=1), "hid")
    return (averages * lax.rsqrt(energy / features + 1e-06)[:, None]).astype(jnp.bfloat16)


def solution(mesh):
    placed = (P("seq", "hid"), P("seq"), P(), P(), P("hid"))
    return jax.shard_map(
        local, mesh=mesh, in_specs=placed, out_specs=P("seq", "hid"), check_vma=False
    )
```

profile of v0, /device:TPU:0, one launch (start us, length us, event | category | flops | bytes accessed | tf_op | source)
XLA Modules:
  0.0 98.1 jit_solution(6189019303345249454)
XLA Ops:
  6.5 0.0 copy-start
  6.5 0.0 copy-start.4
  6.5 0.0 copy-start.2
  6.5 0.0 copy-start.3
  6.5 0.0 copy-start.1
  6.5 0.0 all-reduce.3.cloned.1.call-start
  6.6 0.9 select_reduce_fusion
  7.5 0.7 copy-done
  8.2 1.1 %fusion = f32[32,1024]{1,0:T(8,128)} fusion(bf16[1024,1024]{1,0:T(8,128)(2,1)S(1)} %copy-done, s32[1024]{0:T(1024)S(1)} %select_reduce_fusion), kind=kOutput, calls=%fused_computation.3 | convolution fusion | flops 67141632 | bytes 2232320 | tf_op jit(solution)/shard_map/dot_general | solution.py:22
  9.3 0.0 all-reduce.3.cloned.1.call-update
  9.3 0.0 copy-done.2
  9.3 0.0 copy-done.3
  9.3 0.1 select_reduce_fusion.1
  9.5 0.1 dynamic_slice.3
  9.5 0.0 copy-done.4
  9.6 0.6 dynamic-slice
  10.8 73.1 %all-reduce.3.cloned.1.call-done = f32[32,1024]{1,0:T(8,128)} async-done(((f32[32,1024]{1,0:T(8,128)}), f32[32,1024]{1,0:T(8,128)}) %all-reduce.3.cloned.1.call-update) | async-done | bytes 131088
  83.9 0.0 copy-done.1
  83.9 0.9 multiply_reduce_fusion
  84.9 5.7 %psum.7 = f32[4]{0:T(128)S(1)} all-reduce(f32[4]{0:T(128)S(1)} %get-tuple-element.5), channel_id=1, replica_groups=mesh['seq'=8,'hid'=4] {'hid'}, use_global_device_ids=true, to_apply=%region_4.0 | all-reduce | flops 4 | bytes 32 | tf_op jit(solution)/shard_map/psum | solution.py:29
  90.5 0.7 multiply_convert_fusion
  (2 shorter events, 0.0 us)
Async XLA Ops:
  6.5 1.7 %copy-start = (bf16[1024,1024]{1,0:T(8,128)(2,1)S(1)}, bf16[1024,1024]{1,0:T(8,128)(2,1)}, u32[]{:S(2)}) copy-start(bf16[1024,1024]{1,0:T(8,128)(2,1)} %param.5) | copy-start | bytes 6291460
  6.5 3.0 %copy-start.4 = (u32[32]{0:T(128)S(1)}, u32[32]{0:T(128)}, u32[]{:S(2)}) copy-start(u32[32]{0:T(128)} %constant.23) | copy-start | bytes 388
  6.5 2.8 %copy-start.2 = (s32[32]{0:T(128)S(1)}, s32[32]{0:T(128)}, u32[]{:S(2)}) copy-start(s32[32]{0:T(128)} %param.8) | copy-start | bytes 388
  6.5 2.8 %copy-start.3 = (s32[32]{0:T(128)S(1)}, s32[32]{0:T(128)}, u32[]{:S(2)}) copy-start(s32[32]{0:T(128)} %param.7) | copy-start | bytes 388
  6.5 77.4 %copy-start.1 = (f32[1024]{0:T(1024)S(1)}, f32[1024]{0:T(1024)}, u32[]{:S(2)}) copy-start(f32[1024]{0:T(1024)} %param.9) | copy-start | bytes 12292
  6.5 77.4 %all-reduce.3.cloned.1.call-start = ((), (), s32[]{:S(2)}) async-start(), calls=%async_computation | async-start | bytes 262144
Sparse Core Ops, SparseCore 0:
  10.7 73.1 all-reduce.2
where the time goes:
time: 98.3 us; the launch traced here: 98.1 us
  waiting for transfers between devices  73.1 us (74%)
  between operations  14.1 us (14%)
  blocking collectives  5.66 us (6%)
  other arithmetic  2.68 us (3%)
  local copies, waits for them, and re-layouts  1.34 us (1%)
  matrix products  1.11 us (1%)
    unnamed x2, waiting for transfers between devices  73.1 us
    psum x1, blocking collectives, local(): energy = lax.psum(jnp.sum(averages * averages, axis=1), 'hid')  5.66 us
  transfers between devices with their start and end apart: 1, of which 1 were waited for; matrix products, arithmetic and copies ran while one was open for 1% of the time, Pallas kernels for 0%

commit v1 on v0

v1 whole, which is shorter than its diff:
```python
import functools

import jax
import jax.numpy as jnp
from jax import lax
from jax.experimental import pallas as pl
from jax.experimental.pallas import tpu as pltpu
from jax.sharding import PartitionSpec as P

MESH = pl.DeviceIdType.MESH
LANES = 128


def kernel(
    n_seq, n_hid, chunks, pad,
    hidden_hbm, seg_hbm, len_hbm, slot_hbm, bias_hbm,
    out_ref,
    hidden, seg, lens, slots, bias, parts, landed, mine, squares, squares_in,
    load_sems, small_sems, send_sems, recv_sems, sq_send_sems, sq_recv_sems,
):
    me = lax.axis_index("seq")
    my_hid = lax.axis_index("hid")
    tokens, width = hidden.shape
    docs = lens.shape[1]
    per_owner = docs // n_seq
    step = width // chunks
    features = width * n_hid

    def loader(c):
        cols = pl.ds(c * step, step)
        return pltpu.make_async_copy(hidden_hbm.at[:, cols], hidden.at[:, cols], load_sems.at[c])

    small = [
        pltpu.make_async_copy(src, dst, small_sems.at[i])
        for i, (src, dst) in enumerate(
            ((slot_hbm, slots), (seg_hbm, seg), (len_hbm, lens), (bias_hbm, bias))
        )
    ]
    small[0].start()
    small[1].start()
    loads = [loader(c) for c in range(chunks)]
    for load in loads:
        load.start()
    small[2].start()
    small[3].start()

    barrier = pltpu.get_barrier_semaphore()
    for k in range(1, n_seq):
        pl.semaphore_signal(
            barrier, inc=1, device_id={"seq": lax.rem(me + k, n_seq)}, device_id_type=MESH
        )
    for k in range(1, n_hid):
        pl.semaphore_signal(
            barrier, inc=1, device_id={"hid": lax.rem(my_hid + k, n_hid)}, device_id_type=MESH
        )

    small[0].wait()
    row = lax.broadcasted_iota(jnp.int32, (n_seq * pad, 1), 0)
    inner = row % pad
    row_slot = jnp.where(inner < per_owner, (row // pad) * per_owner + inner, -1)
    doc_iota = lax.broadcasted_iota(jnp.int32, (1, docs), 1).astype(jnp.float32)
    found = jnp.where(row_slot == slots[...], doc_iota + 1.0, 0.0)
    row_doc = jnp.sum(found, axis=1, keepdims=True).astype(jnp.int32) - 1
    small[1].wait()
    picker = jnp.concatenate(
        [
            jnp.where(row_doc == seg[k : k + 1, :], 1.0, 0.0).astype(jnp.bfloat16)
            for k in range(tokens // LANES)
        ],
        axis=1,
    )

    def sender(c, k):
        cols = pl.ds(c * step, step)
        peer = lax.rem(me + k, n_seq)
        return pltpu.make_async_remote_copy(
            src_ref=parts.at[peer, :, cols],
            dst_ref=landed.at[k - 1, :, cols],
            send_sem=send_sems.at[c, k - 1],
            recv_sem=recv_sems.at[c, k - 1],
            device_id={"seq": peer},
            device_id_type=MESH,
        )

    order = sorted(range(1, n_seq), key=lambda k: -min(k, n_seq - k))
    for c in range(chunks):
        cols = pl.ds(c * step, step)
        loads[c].wait()
        product = jnp.dot(picker, hidden[:, cols], preferred_element_type=jnp.float32)
        for p in range(n_seq):
            parts[p, :, cols] = product[p * pad : p * pad + per_owner, :]
        if c == 0:
            pl.semaphore_wait(barrier, n_seq - 1 + n_hid - 1)
        for k in order:
            sender(c, k).start()

    small[2].wait()
    small[3].wait()
    wanted = lax.broadcasted_iota(jnp.int32, (per_owner, 1), 0) + me * per_owner
    my_len = jnp.sum(
        jnp.where(wanted == slots[...], lens[...].astype(jnp.float32), 0.0), axis=1, keepdims=True
    )

    lane_sq = jnp.zeros((per_owner, LANES), jnp.float32)
    for c in range(chunks):
        cols = pl.ds(c * step, step)
        total = parts[me, :, cols]
        for k in order[::-1]:
            sender(c, k).wait_recv()
            total = total + landed[k - 1, :, cols]
        averages = total / my_len + bias[:, cols]
        mine[:, cols] = averages
        for j in range(step // LANES):
            piece = averages[:, j * LANES : (j + 1) * LANES]
            lane_sq = lane_sq + piece * piece
    squares[...] = lane_sq

    sq_copies = []
    for k in range(1, n_hid):
        copy = pltpu.make_async_remote_copy(
            src_ref=squares,
            dst_ref=squares_in.at[k - 1],
            send_sem=sq_send_sems.at[k - 1],
            recv_sem=sq_recv_sems.at[k - 1],
            device_id={"hid": lax.rem(my_hid + k, n_hid)},
            device_id_type=MESH,
        )
        copy.start()
        sq_copies.append(copy)
    for c in range(chunks):
        for k in order:
            sender(c, k).wait_send()
    for k in range(1, n_hid):
        sq_copies[k - 1].wait_recv()
        lane_sq = lane_sq + squares_in[k - 1]
    energy = jnp.sum(lane_sq, axis=1, keepdims=True) / features
    out_ref[...] = (mine[...] * lax.rsqrt(energy + 1e-06)).astype(jnp.bfloat16)
    for copy in sq_copies:
        copy.wait_send()


def local(n_seq, n_hid, hidden, seg_ids, lengths, owner_slot, pool_bias):
    tokens, width = hidden.shape
    docs = lengths.shape[0]
    per_owner = docs // n_seq
    pad = -(-per_owner // 8) * 8
    chunks = 4
    f32 = jnp.float32
    dma = pltpu.SemaphoreType.DMA
    return pl.pallas_call(
        functools.partial(kernel, n_seq, n_hid, chunks, pad),
        out_shape=jax.ShapeDtypeStruct((per_owner, width), jnp.bfloat16),
        in_specs=[pl.BlockSpec(memory_space=pl.ANY)] * 5,
        out_specs=pl.BlockSpec(memory_space=pltpu.VMEM),
        scratch_shapes=[
            pltpu.VMEM((tokens, width), jnp.bfloat16),
            pltpu.VMEM((tokens // LANES, LANES), jnp.int32),
            pltpu.VMEM((1, docs), jnp.int32),
            pltpu.VMEM((1, docs), jnp.int32),
            pltpu.VMEM((1, width), f32),
            pltpu.VMEM((n_seq, per_owner, width), f32),
            pltpu.VMEM((n_seq - 1, per_owner, width), f32),
            pltpu.VMEM((per_owner, width), f32),
            pltpu.VMEM((per_owner, LANES), f32),
            pltpu.VMEM((n_hid - 1, per_owner, LANES), f32),
            dma((chunks,)),
            dma((4,)),
            dma((chunks, n_seq - 1)),
            dma((chunks, n_seq - 1)),
            dma((n_hid - 1,)),
            dma((n_hid - 1,)),
        ],
        compiler_params=pltpu.CompilerParams(collective_id=0, has_side_effects=True),
    )(
        hidden,
        seg_ids.reshape(tokens // LANES, LANES),
        lengths.reshape(1, docs),
        owner_slot.reshape(1, docs),
        pool_bias.reshape(1, width),
    )


def solution(mesh):
    placed = (P("seq", "hid"), P("seq"), P(), P(), P("hid"))
    return jax.shard_map(
        functools.partial(local, mesh.shape["seq"], mesh.shape["hid"]),
        mesh=mesh,
        in_specs=placed,
        out_specs=P("seq", "hid"),
        check_vma=False,
    )
```

time: 98.3 us -> 16.2 us (0.16)
  waiting for transfers between devices: 73.1 us -> 0 us
  Pallas kernels: 0 us -> 14.6 us
  between operations: 14.1 us -> 0.01 us
  blocking collectives: 5.66 us -> 0 us
  other arithmetic: 2.68 us -> 0 us
  matrix products: 1.11 us -> 0 us
    unnamed x2 -> x0, waiting for transfers between devices: 73.1 us -> none
    pallas_call x0 -> x1, Pallas kernels: none -> 14.6 us  [local(): pl.pallas_call(functools.partial(kernel, n_seq, n_hid, chunks, pad), out_...]
    psum x1 -> x0, blocking collectives: 5.66 us -> none  [local(): energy = lax.psum(jnp.sum(averages * averages, axis=1), 'hid')]
    reduce_sum x3 -> x0, other arithmetic: 1.99 us -> none  [the longest x1 0.95 us: local(): energy = lax.psum(jnp.sum(averages * averages, axis=1), 'hid')]
    dot_general x1 -> x0, matrix products: 1.11 us -> none  [local(): jnp.dot(picker, hidden, preferred_element_type=jnp.float32)]
  transfers between devices with their start and end apart: 1 -> 0, of which waited for: 1 -> 0; matrix products, arithmetic and copies ran while one was open for 1% -> 0% of each run, Pallas kernels for 0% -> 0%
where the time goes in v1:
time: 16.2 us; the launch traced here: 16 us
  Pallas kernels  14.6 us (90%)
  local copies, waits for them, and re-layouts  1.3 us (8%)
    pallas_call x1, Pallas kernels, local(): pl.pallas_call(functools.partial(kernel, n_seq, n_hid, chunks, pad), out_...  14.6 us
    unnamed x1, local copies, waits for them, and re-layouts  1.3 us

profile of v1, /device:TPU:0, one launch (start us, length us, event | category | flops | bytes accessed | tf_op | source)
XLA Modules:
  0.0 16.0 jit_solution(17850874952682996684)
XLA Ops:
  0.0 14.6 %shard_map.55 = bf16[4,1024]{1,0:T(4,128)(2,1)} custom-call(bf16[1024,1024]{1,0:T(8,128)(2,1)} %hidden_hbm.1, s32[8,128]{1,0:T(8,128)} %bitcast.4, s32[1,32]{1,0:T(1,128)} %bitcast.6, s32[1,32]{1,0:T(1,128)} %bitcast.7, f32[1,1024]{1,0:T(1,128)} %bitcast.5), custom_call_target="tpu_custom_call" | custom-call | tf_op jit(solution)/shard_map/pallas_call | solution.py:150
  14.7 1.3 %copy.7 = bf16[4,1024]{1,0:T(4,128)(2,1)} copy(bf16[4,1024]{1,0:T(4,128)(2,1)} %shard_map.55) | data formatting | bytes 16384

commit v2 on v1

--- a/solution.py
+++ b/solution.py
@@ -15,8 +15,8 @@
     n_seq, n_hid, chunks, pad,
     hidden_hbm, seg_hbm, len_hbm, slot_hbm, bias_hbm,
     out_ref,
-    hidden, seg, lens, slots, bias, parts, landed, mine, squares, squares_in,
-    load_sems, small_sems, send_sems, recv_sems, sq_send_sems, sq_recv_sems,
+    hidden, seg, lens, slots, bias, parts, landed, squares, squares_in,
+    load_sems, small_sems, send_sem, recv_sem, sq_send_sem, sq_recv_sem,
 ):
     me = lax.axis_index("seq")
     my_hid = lax.axis_index("hid")
@@ -25,6 +25,15 @@
     per_owner = docs // n_seq
     step = width // chunks
     features = width * n_hid
+    order = sorted(range(1, n_seq), key=lambda k: -min(k, n_seq - k))
+    peers = {k: lax.rem(me + k, n_seq) for k in order}
+    hid_peers = {k: lax.rem(my_hid + k, n_hid) for k in range(1, n_hid)}
+
+    barrier = pltpu.get_barrier_semaphore()
+    for k in order:
+        pl.semaphore_signal(barrier, inc=1, device_id={"seq": peers[k]}, device_id_type=MESH)
+    for k in range(1, n_hid):
+        pl.semaphore_signal(barrier, inc=1, device_id={"hid": hid_peers[k]}, device_id_type=MESH)
 
     def loader(c):
         cols = pl.ds(c * step, step)
@@ -44,16 +53,6 @@
     small[2].start()
     small[3].start()
 
-    barrier = pltpu.get_barrier_semaphore()
-    for k in range(1, n_seq):
-        pl.semaphore_signal(
-            barrier, inc=1, device_id={"seq": lax.rem(me + k, n_seq)}, device_id_type=MESH
-        )
-    for k in range(1, n_hid):
-        pl.semaphore_signal(
-            barrier, inc=1, device_id={"hid": lax.rem(my_hid + k, n_hid)}, device_id_type=MESH
-        )
-
     small[0].wait()
     row = lax.broadcasted_iota(jnp.int32, (n_seq * pad, 1), 0)
     inner = row % pad
@@ -72,17 +71,16 @@
 
     def sender(c, k):
         cols = pl.ds(c * step, step)
-        peer = lax.rem(me + k, n_seq)
+        peer = peers[k]
         return pltpu.make_async_remote_copy(
             src_ref=parts.at[peer, :, cols],
             dst_ref=landed.at[k - 1, :, cols],
-            send_sem=send_sems.at[c, k - 1],
-            recv_sem=recv_sems.at[c, k - 1],
+            send_sem=send_sem,
+            recv_sem=recv_sem,
             device_id={"seq": peer},
             device_id_type=MESH,
         )
 
-    order = sorted(range(1, n_seq), key=lambda k: -min(k, n_seq - k))
     for c in range(chunks):
         cols = pl.ds(c * step, step)
         loads[c].wait()
@@ -101,42 +99,33 @@
         jnp.where(wanted == slots[...], lens[...].astype(jnp.float32), 0.0), axis=1, keepdims=True
     )
 
+    pltpu.make_async_copy(landed, landed, recv_sem).wait()
+    total = parts[me]
+    for k in range(n_seq - 1):
+        total = total + landed[k]
+    averages = total / my_len + bias[...]
     lane_sq = jnp.zeros((per_owner, LANES), jnp.float32)
-    for c in range(chunks):
-        cols = pl.ds(c * step, step)
-        total = parts[me, :, cols]
-        for k in order[::-1]:
-            sender(c, k).wait_recv()
-            total = total + landed[k - 1, :, cols]
-        averages = total / my_len + bias[:, cols]
-        mine[:, cols] = averages
-        for j in range(step // LANES):
-            piece = averages[:, j * LANES : (j + 1) * LANES]
-            lane_sq = lane_sq + piece * piece
+    for j in range(width // LANES):
+        piece = averages[:, j * LANES : (j + 1) * LANES]
+        lane_sq = lane_sq + piece * piece
     squares[...] = lane_sq
 
-    sq_copies = []
     for k in range(1, n_hid):
-        copy = pltpu.make_async_remote_copy(
+        pltpu.make_async_remote_copy(
             src_ref=squares,
             dst_ref=squares_in.at[k - 1],
-            send_sem=sq_send_sems.at[k - 1],
-            recv_sem=sq_recv_sems.at[k - 1],
-            device_id={"hid": lax.rem(my_hid + k, n_hid)},
+            send_sem=sq_send_sem,
+            recv_sem=sq_recv_sem,
+            device_id={"hid": hid_peers[k]},
             device_id_type=MESH,
-        )
-        copy.start()
-        sq_copies.append(copy)
-    for c in range(chunks):
-        for k in order:
-            sender(c, k).wait_send()
-    for k in range(1, n_hid):
-        sq_copies[k - 1].wait_recv()
-        lane_sq = lane_sq + squares_in[k - 1]
+        ).start()
+    pltpu.make_async_copy(landed, landed, send_sem).wait()
+    pltpu.make_async_copy(squares_in, squares_in, sq_recv_sem).wait()
+    for k in range(n_hid - 1):
+        lane_sq = lane_sq + squares_in[k]
     energy = jnp.sum(lane_sq, axis=1, keepdims=True) / features
-    out_ref[...] = (mine[...] * lax.rsqrt(energy + 1e-06)).astype(jnp.bfloat16)
-    for copy in sq_copies:
-        copy.wait_send()
+    out_ref[...] = (averages * lax.rsqrt(energy + 1e-06)).astype(jnp.bfloat16)
+    pltpu.make_async_copy(squares_in, squares_in, sq_send_sem).wait()
 
 
 def local(n_seq, n_hid, hidden, seg_ids, lengths, owner_slot, pool_bias):
@@ -149,7 +138,7 @@
     dma = pltpu.SemaphoreType.DMA
     return pl.pallas_call(
         functools.partial(kernel, n_seq, n_hid, chunks, pad),
-        out_shape=jax.ShapeDtypeStruct((per_owner, width), jnp.bfloat16),
+        out_shape=pltpu.VMEM((per_owner, width), jnp.bfloat16),
         in_specs=[pl.BlockSpec(memory_space=pl.ANY)] * 5,
         out_specs=pl.BlockSpec(memory_space=pltpu.VMEM),
         scratch_shapes=[
@@ -160,15 +149,14 @@
             pltpu.VMEM((1, width), f32),
             pltpu.VMEM((n_seq, per_owner, width), f32),
             pltpu.VMEM((n_seq - 1, per_owner, width), f32),
-            pltpu.VMEM((per_owner, width), f32),
             pltpu.VMEM((per_owner, LANES), f32),
             pltpu.VMEM((n_hid - 1, per_owner, LANES), f32),
             dma((chunks,)),
             dma((4,)),
-            dma((chunks, n_seq - 1)),
-            dma((chunks, n_seq - 1)),
-            dma((n_hid - 1,)),
-            dma((n_hid - 1,)),
+            dma(()),
+            dma(()),
+            dma(()),
+            dma(()),
         ],
         compiler_params=pltpu.CompilerParams(collective_id=0, has_side_effects=True),
     )(

time: 16.2 us -> 14.3 us (0.88)
  Pallas kernels: 14.6 us -> 13.5 us
  local copies, waits for them, and re-layouts: 1.3 us -> 0.6 us
    pallas_call x1, Pallas kernels: 14.6 us -> 13.5 us  [local(): pl.pallas_call(functools.partial(kernel, n_seq, n_hid, chunks, pad), out_...]
    unnamed x1, local copies, waits for them, and re-layouts: 1.3 us -> 0.6 us
where the time goes in v2:
time: 14.3 us; the launch traced here: 14.2 us
  Pallas kernels  13.5 us (94%)
  local copies, waits for them, and re-layouts  0.6 us (4%)
    pallas_call x1, Pallas kernels, local(): pl.pallas_call(functools.partial(kernel, n_seq, n_hid, chunks, pad), out_...  13.5 us
    unnamed x1, local copies, waits for them, and re-layouts  0.6 us

profile of v2, /device:TPU:0, one launch (start us, length us, event | category | flops | bytes accessed | tf_op | source)
XLA Modules:
  0.0 14.2 jit_solution(13902904482930764092)
XLA Ops:
  0.0 13.5 %shard_map.55 = bf16[4,1024]{1,0:T(4,128)(2,1)S(1)} custom-call(bf16[1024,1024]{1,0:T(8,128)(2,1)} %hidden_hbm.1, s32[8,128]{1,0:T(8,128)} %bitcast.4, s32[1,32]{1,0:T(1,128)} %bitcast.6, s32[1,32]{1,0:T(1,128)} %bitcast.7, f32[1,1024]{1,0:T(1,128)} %bitcast.5), custom_call_target="tpu_custom_call" | custom-call | tf_op jit(solution)/shard_map/pallas_call | solution.py:139
  13.6 0.6 %copy.7 = bf16[4,1024]{1,0:T(4,128)(2,1)} copy(bf16[4,1024]{1,0:T(4,128)(2,1)S(1)} %shard_map.55) | data formatting | bytes 16384

commit v3 on v2

--- a/solution.py
+++ b/solution.py
@@ -12,7 +12,7 @@
 
 
 def kernel(
-    n_seq, n_hid, chunks, pad,
+    n_seq, n_hid, chunks, urgent, pad,
     hidden_hbm, seg_hbm, len_hbm, slot_hbm, bias_hbm,
     out_ref,
     hidden, seg, lens, slots, bias, parts, landed, squares, squares_in,
@@ -25,15 +25,9 @@
     per_owner = docs // n_seq
     step = width // chunks
     features = width * n_hid
-    order = sorted(range(1, n_seq), key=lambda k: -min(k, n_seq - k))
-    peers = {k: lax.rem(me + k, n_seq) for k in order}
+    peers = [jnp.where(j < me, j, j + 1) for j in range(n_seq - 1)]
+    slot_there = [jnp.where(j < me, me - 1, me) for j in range(n_seq - 1)]
     hid_peers = {k: lax.rem(my_hid + k, n_hid) for k in range(1, n_hid)}
-
-    barrier = pltpu.get_barrier_semaphore()
-    for k in order:
-        pl.semaphore_signal(barrier, inc=1, device_id={"seq": peers[k]}, device_id_type=MESH)
-    for k in range(1, n_hid):
-        pl.semaphore_signal(barrier, inc=1, device_id={"hid": hid_peers[k]}, device_id_type=MESH)
 
     def loader(c):
         cols = pl.ds(c * step, step)
@@ -53,6 +47,12 @@
     small[2].start()
     small[3].start()
 
+    barrier = pltpu.get_barrier_semaphore()
+    for peer in peers:
+        pl.semaphore_signal(barrier, inc=1, device_id={"seq": peer}, device_id_type=MESH)
+    for k in range(1, n_hid):
+        pl.semaphore_signal(barrier, inc=1, device_id={"hid": hid_peers[k]}, device_id_type=MESH)
+
     small[0].wait()
     row = lax.broadcasted_iota(jnp.int32, (n_seq * pad, 1), 0)
     inner = row % pad
@@ -69,17 +69,15 @@
         axis=1,
     )
 
-    def sender(c, k):
-        cols = pl.ds(c * step, step)
-        peer = peers[k]
-        return pltpu.make_async_remote_copy(
-            src_ref=parts.at[peer, :, cols],
-            dst_ref=landed.at[k - 1, :, cols],
+    def send(cols, j):
+        pltpu.make_async_remote_copy(
+            src_ref=parts.at[peers[j], :, cols],
+            dst_ref=landed.at[slot_there[j], :, cols],
             send_sem=send_sem,
             recv_sem=recv_sem,
-            device_id={"seq": peer},
+            device_id={"seq": peers[j]},
             device_id_type=MESH,
-        )
+        ).start()
 
     for c in range(chunks):
         cols = pl.ds(c * step, step)
@@ -89,8 +87,10 @@
             parts[p, :, cols] = product[p * pad : p * pad + per_owner, :]
         if c == 0:
             pl.semaphore_wait(barrier, n_seq - 1 + n_hid - 1)
-        for k in order:
-            sender(c, k).start()
+        for j in range(urgent):
+            send(cols, j)
+    for j in range(urgent, n_seq - 1):
+        send(pl.ds(0, width), j)
 
     small[2].wait()
     small[3].wait()
@@ -133,11 +133,12 @@
     docs = lengths.shape[0]
     per_owner = docs // n_seq
     pad = -(-per_owner // 8) * 8
-    chunks = 4
+    chunks = 2
+    urgent = max(1, n_seq // 4)
     f32 = jnp.float32
     dma = pltpu.SemaphoreType.DMA
     return pl.pallas_call(
-        functools.partial(kernel, n_seq, n_hid, chunks, pad),
+        functools.partial(kernel, n_seq, n_hid, chunks, urgent, pad),
         out_shape=pltpu.VMEM((per_owner, width), jnp.bfloat16),
         in_specs=[pl.BlockSpec(memory_space=pl.ANY)] * 5,
         out_specs=pl.BlockSpec(memory_space=pltpu.VMEM),

time: 14.3 us -> 13.7 us (0.958)
  Pallas kernels: 13.5 us -> 12.9 us
    pallas_call x1, Pallas kernels: 13.5 us -> 12.9 us  [local(): pl.pallas_call(functools.partial(kernel, n_seq, n_hid, chunks, urgent, pa...]
where the time goes in v3:
time: 13.7 us; the launch traced here: 13.5 us
  Pallas kernels  12.9 us (94%)
  local copies, waits for them, and re-layouts  0.6 us (4%)
    pallas_call x1, Pallas kernels, local(): pl.pallas_call(functools.partial(kernel, n_seq, n_hid, chunks, urgent, pa...  12.9 us
    unnamed x1, local copies, waits for them, and re-layouts  0.6 us

profile of v3, /device:TPU:0, one launch (start us, length us, event | category | flops | bytes accessed | tf_op | source)
XLA Modules:
  0.0 13.5 jit_solution(13235726092053567432)
XLA Ops:
  0.0 12.9 %shard_map.55 = bf16[4,1024]{1,0:T(4,128)(2,1)S(1)} custom-call(bf16[1024,1024]{1,0:T(8,128)(2,1)} %hidden_hbm.1, s32[8,128]{1,0:T(8,128)} %bitcast.4, s32[1,32]{1,0:T(1,128)} %bitcast.6, s32[1,32]{1,0:T(1,128)} %bitcast.7, f32[1,1024]{1,0:T(1,128)} %bitcast.5), custom_call_target="tpu_custom_call" | custom-call | tf_op jit(solution)/shard_map/pallas_call | solution.py:140
  12.9 0.6 %copy.7 = bf16[4,1024]{1,0:T(4,128)(2,1)} copy(bf16[4,1024]{1,0:T(4,128)(2,1)S(1)} %shard_map.55) | data formatting | bytes 16384

commit v4 on v3

--- a/solution.py
+++ b/solution.py
@@ -42,8 +42,15 @@
     small[0].start()
     small[1].start()
     loads = [loader(c) for c in range(chunks)]
-    for load in loads:
-        load.start()
+    pieces = 4
+    rows = tokens // pieces
+    for c in range(chunks):
+        cols = pl.ds(c * step, step)
+        for r in range(pieces):
+            part = pl.ds(r * rows, rows)
+            pltpu.make_async_copy(
+                hidden_hbm.at[part, cols], hidden.at[part, cols], load_sems.at[c]
+            ).start()
     small[2].start()
     small[3].start()
 

time: 13.7 us -> 13.6 us (level)
  no operation moved by 1% of the time
where the time goes in v4:
time: 13.6 us; the launch traced here: 13.4 us
  Pallas kernels  12.8 us (94%)
  local copies, waits for them, and re-layouts  0.6 us (4%)
    pallas_call x1, Pallas kernels, local(): pl.pallas_call(functools.partial(kernel, n_seq, n_hid, chunks, urgent, pa...  12.8 us
    unnamed x1, local copies, waits for them, and re-layouts  0.6 us

profile of v4, /device:TPU:0, one launch (start us, length us, event | category | flops | bytes accessed | tf_op | source)
XLA Modules:
  0.0 13.4 jit_solution(2006705680421338349)
XLA Ops:
  0.0 12.8 %shard_map.55 = bf16[4,1024]{1,0:T(4,128)(2,1)S(1)} custom-call(bf16[1024,1024]{1,0:T(8,128)(2,1)} %hidden_hbm.1, s32[8,128]{1,0:T(8,128)} %bitcast.4, s32[1,32]{1,0:T(1,128)} %bitcast.6, s32[1,32]{1,0:T(1,128)} %bitcast.7, f32[1,1024]{1,0:T(1,128)} %bitcast.5), custom_call_target="tpu_custom_call" | custom-call | tf_op jit(solution)/shard_map/pallas_call | solution.py:147
  12.8 0.6 %copy.7 = bf16[4,1024]{1,0:T(4,128)(2,1)} copy(bf16[4,1024]{1,0:T(4,128)(2,1)S(1)} %shard_map.55) | data formatting | bytes 16384
